TPU v7x, 128 devices: a whole 4x4x4 slice. The times are simulated.
128 devices in a mesh: ta: 64 (over y, x, z), gz: 2 (over core).
Axes of the slice: x: 4, y: 4, z: 4, core: 2. Of those that a mesh axis runs over, the one named last changes fastest.
Arguments:
- propagator: float32 [2, 12, 12, 64, 13824], P(None, None, None, 'ta', 'gz'), may hold values from -6 to 6
- backward: float32 [2, 12, 12, 64, 13824], P(None, None, None, 'ta', 'gz'), may hold values from -6 to 6
- sink_time: int32 [1], replicated, may hold values from 0 to 63
- source_position: int32 [3], replicated, may hold values from 0 to 23
- momenta: int32 [27, 3], replicated, may hold values from -3 to 3
- gamma_table: int32 [16], replicated, may hold values from 0 to 15, each once
Outputs:
- correlator: float32 [2, 64, 16, 27], P(None, 'ta', 'gz')
Inputs may be any that keep to these rules, and one draw needn't show every extreme that they name: `gamma_table`: each of 0 to 15 appears exactly once.
All inputs are finite; a program needn't handle non-finite values.
Results may differ from a plain program's by a relative error of at most 0.00007.
Values sent between devices are 32-bit elements; how exact they have to be, the bound alone decides.
A program may use at most 192 MiB of HBM per device.

v0:
```python
import functools
import itertools
import math

import jax
import jax.numpy as jnp
import numpy as np
from jax import lax
from jax.experimental import pallas as pl
from jax.experimental.pallas import tpu as pltpu
from jax.sharding import PartitionSpec as P

L = 24
NG = 16
NP = 27
CHUNKS = 7
LAG = 6
PACKETS = 4 * CHUNKS
DEPTH = 7
SLOTS = PACKETS + DEPTH * LAG
SENDS = SLOTS - LAG
FIRST = DEPTH * LAG + 4
END = FIRST + PACKETS
OUT_RING = 4
SEM_RING = 16
STEPS = ((1, 0, 0), (-1, 0, 0), (0, 1, 0), (0, -1, 0), (0, 0, 1), (0, 0, -1))
TREE_STEPS = (0, 3, 4, 1, 2, 5)
MESH = pl.DeviceIdType.MESH
F32 = jnp.float32


def moved(v, step, sign=1):
    return tuple((a + sign * b) % 4 for a, b in zip(v, step))


def turned(v):
    return tuple((-c) % 4 for c in (v[2], v[0], v[1]))


def turned_step(d):
    return tuple(-c for c in (d[2], d[0], d[1]))


@functools.cache
def tree_words():
    nodes = list(itertools.product(range(4), repeat=3))
    root, child = (0, 0, 0), (1, 0, 0)

    def level(v):
        return sum(min((a - b) % 4, (b - a) % 4) for a, b in zip(v, child))

    def orbit(tail, step):
        while step != (1, 0, 0):
            tail, step = turned(tail), turned_step(step)
        return tail

    taken = orbit(root, (1, 0, 0))
    options = {
        v: [
            (orbit(moved(v, d, -1), d), d)
            for d in STEPS
            if moved(v, d, -1) != root and level(moved(v, d, -1)) < level(v)
        ]
        for v in nodes
        if v not in (root, child)
    }
    match = {}

    def augment(v, seen):
        for key, d in options[v]:
            if key == taken or key in seen:
                continue
            seen.add(key)
            if key not in match or augment(match[key][0], seen):
                match[key] = (v, d)
                return True
        return False

    for v in options:
        assert augment(v, set())
    into = {child: (1, 0, 0)}
    for v, d in match.values():
        into[v] = d
    depth = {root: 0}

    def depth_of(v):
        if v not in depth:
            depth[v] = depth_of(moved(v, into[v], -1)) + 1
        return depth[v]

    edges = [(v, d) for v, d in into.items()]
    depths = {v: depth_of(v) for v in nodes}
    words = np.zeros((3, 64), np.int32)

    def number(v):
        return (v[0] * 4 + v[1]) * 4 + v[2]

    seen_edges = set()
    for k in range(6):
        assert STEPS.index([d for v, d in edges if moved(v, d, -1) == root][0]) == TREE_STEPS[k]
        for v, d in edges:
            n, j = number(v), STEPS.index(d)
            tail = number(moved(v, d, -1))
            assert (tail, j) not in seen_edges
            seen_edges.add((tail, j))
            words[0, n] |= j << (3 * k)
            words[1, tail] |= k << (3 * j)
        for v, n_hops in depths.items():
            assert n_hops <= DEPTH
            words[2, number(v)] |= n_hops << (3 * k)
        edges = [(turned(v), turned_step(d)) for v, d in edges]
        depths = {turned(v): n_hops for v, n_hops in depths.items()}
    return words.reshape(-1)


def source_pairs():
    return [(i, j) for i in range(12) for j in range(i, 12)]


PAIRS = source_pairs()
PAIR_NUMBER = {p: n for n, p in enumerate(PAIRS)}


def pair_number(i, j):
    return PAIR_NUMBER[(min(i, j), max(i, j))]


def kernel(
    prop, back, words, sink, origin, momenta, gtab, out,
    sv, hv, own, inbox, stream, outbox, sig, hsum, ssum, macc, kbuf, ph_hi, ph_lo,
    mom, acc, cbuf, ex, rx,
    s_sem, h_sem, send_sem, recv_sem, ex_send, ex_recv,
):
    ta = lax.axis_index("ta")
    gz = lax.axis_index("gz")
    cy, cx, cz = ta // 16, (ta // 4) % 4, ta % 4

    def load(src, dst, sem, c):
        sites = 1024 if c < CHUNKS - 1 else 768
        return pltpu.make_async_copy(
            src.at[:, :, :, :, pl.ds(1024 * c, sites)],
            dst.at[c, :, :, :, :, pl.ds(0, sites)],
            sem.at[c],
        )

    for c in range(CHUNKS):
        load(prop, sv, s_sem, c).start()
    for c in range(CHUNKS):
        load(back, hv, h_sem, c).start()

    def neighbour(d):
        x, y, z = STEPS[d]
        return ((cy + y + 4) % 4 * 4 + (cx + x + 4) % 4) * 4 + (cz + z + 4) % 4

    barrier = pltpu.get_barrier_semaphore()
    for d in range(6):
        pl.semaphore_signal(barrier, inc=1, device_id=(neighbour(d), gz), device_id_type=MESH)
    pl.semaphore_signal(barrier, inc=1, device_id=(ta, 1 - gz), device_id_type=MESH)

    root = sink[0]
    rel_x = (cx - root // 4 % 4 + 4) % 4
    rel_y = (cy - root // 16 + 4) % 4
    rel_z = (cz - root % 4 + 4) % 4
    rel = (rel_x * 4 + rel_y) * 4 + rel_z
    is_root = rel == 0
    into_word, from_word, depth_word = words[rel], words[64 + rel], words[128 + rel]
    into = [(into_word >> (3 * k)) & 7 for k in range(6)]
    out_of = [(from_word >> (3 * d)) & 7 for d in range(6)]
    base = [((depth_word >> (3 * k)) & 7) * (13 * LAG // 2) for k in range(6)]

    def source(c, part):
        lo, hi = ((0, 4), (4, 7), (7, 10), (10, 13))[part]
        for k in range(6):
            for n in range(lo, hi):
                i, j = PAIRS[13 * k + n]
                re = im = None
                for m in range(12):
                    a, b = sv[c, 0, i, m], sv[c, 1, i, m]
                    if i == j:
                        r, q = a * a - b * b, a * b
                        q = q + q
                    else:
                        e, f = sv[c, 0, j, m], sv[c, 1, j, m]
                        r, q = a * e - b * f, a * f + b * e
                    re = r if re is None else re + r
                    im = q if im is None else im + q
                own[c, k, 2 * n] = re
                own[c, k, 2 * n + 1] = im

    def message(parity, s, d):
        tiles = 7 - parity
        return pltpu.make_async_remote_copy(
            src_ref=outbox.at[s % OUT_RING, d, pl.ds(0, tiles)],
            dst_ref=inbox.at[s + LAG, d, pl.ds(0, tiles)],
            send_sem=send_sem.at[s % OUT_RING, d],
            recv_sem=recv_sem.at[s % SEM_RING, d],
            device_id=(neighbour(d), gz),
            device_id_type=MESH,
        )

    def chosen(s, k, i):
        best = inbox[s, 5, i]
        for d in range(5):
            best = jnp.where(into[k] == d, inbox[s, d, i], best)
        return best

    def relay(s, parity):
        tiles = 7 - parity
        flat = s // 2 * 13 + 7 * parity
        c, u = s // 4, s % 4
        first = u // 2 * 13 + 7 * parity

        @pl.when(s >= LAG)
        def _():
            for d in range(6):
                message(parity, s - LAG, d).wait_recv()

        @pl.when(s < LAG)
        def _():
            for k in range(6):
                for i in range(tiles):
                    stream[k, flat + i] = own[c, k, first + i]

        @pl.when((s >= LAG) & (s < PACKETS))
        def _():
            for i in range(tiles):
                for k in range(6):
                    stream[k, flat + i] = jnp.where(is_root, own[c, k, first + i], chosen(s, k, i))

        @pl.when(s >= PACKETS)
        def _():
            for i in range(tiles):
                for k in range(6):
                    stream[k, flat + i] = chosen(s, k, i)

        @pl.when(s < SENDS)
        def _():
            @pl.when(s >= OUT_RING)
            def _():
                for d in range(6):
                    message(parity, s - OUT_RING, d).wait_send()

            for d in range(6):
                k = jnp.where(is_root, TREE_STEPS.index(d), out_of[d])
                for i in range(tiles):
                    outbox[s % OUT_RING, d, i] = stream[k, flat + i]
            for d in range(6):
                message(parity, s, d).start()

    def phases(c):
        lane = lax.broadcasted_iota(jnp.int32, (32, 128), 1).astype(F32)
        px, py, pz = mom[0], mom[1], mom[2]
        start = (gz * 6912 + c * 1024).astype(F32)
        for pair in range(4):
            for half in range(2):
                site = lane + (start + (256.0 * pair + 128.0 * half))
                z = jnp.floor((site + 0.5) * (1.0 / 576.0))
                rest = site - z * 576.0
                x = jnp.floor((rest + 0.5) * (1.0 / 24.0))
                y = rest - x * 24.0
                wave = px * (x - ox) + py * (y - oy) + pz * (z - oz)
                wave = wave - 24.0 * jnp.floor((wave + 0.5) * (1.0 / 24.0))
                angle = wave * (2.0 * math.pi / L)
                for row, value in ((0, jnp.cos(angle)), (32, -jnp.sin(angle))):
                    hi = value.astype(jnp.bfloat16)
                    at = (c, pair, pl.ds(row, 32), pl.ds(128 * half, 128))
                    ph_hi[at] = hi
                    ph_lo[at] = (value - hi.astype(F32)).astype(jnp.bfloat16)

    ox, oy, oz = (origin[i].astype(F32) for i in range(3))

    def unpack(c):
        for k in range(6):
            for n in range(13):
                at = base[k] + c * 26 + 2 * n
                re, im = stream[k, at], stream[k, at + 1]
                sig[0, 13 * k + n] = re
                sig[1, 13 * k + n] = im - re
                sig[2, 13 * k + n] = im + re
        for i in range(12):
            for m in range(12):
                ssum[i, m] = sv[c, 0, i, m] + sv[c, 1, i, m]

    def contract(c, al):
        for a in range(3):
            for m in range(12):
                hsum[a, m] = hv[c, 0, 3 * al + a, m] + hv[c, 1, 3 * al + a, m]
        total = [[None] * 3 for _ in range(4)]

        def plus(x, y):
            return y if x is None else x + y

        for block in range(4):
            columns = range(3 * block, 3 * block + 3)
            part = {(a, m): [None] * 3 for a in range(3) for m in columns}
            for k in range(12):
                left = [
                    (hsum[a, k], hv[c, 0, 3 * al + a, k], hv[c, 1, 3 * al + a, k])
                    for a in range(3)
                ]
                for m in columns:
                    n = pair_number(k, m)
                    right = (sig[0, n], sig[1, n], sig[2, n])
                    for a in range(3):
                        for t in range(3):
                            part[a, m][t] = plus(part[a, m][t], left[a][t] * right[t])
            for a in range(3):
                for m in columns:
                    k1, k2, k3 = part[a, m]
                    br, bi = k1 - k3, k1 + k2
                    bound = (br, br + bi, br - bi)
                    for be in range(4):
                        row = 3 * be + a
                        forward = (ssum[row, m], sv[c, 0, row, m], sv[c, 1, row, m])
                        for t in range(3):
                            total[be][t] = plus(total[be][t], forward[t] * bound[t])
        for be in range(4):
            macc[0, be, al] = total[be][0] - total[be][2]
            macc[1, be, al] = total[be][0] - total[be][1]

    def add(p, q):
        return (p[0] + q[0], p[1] + q[1])

    def sub(p, q):
        return (p[0] - q[0], p[1] - q[1])

    def pauli(m):
        d = sub(m[0][1], m[1][0])
        return [add(m[0][0], m[1][1]), add(m[1][0], m[0][1]), (-d[1], d[0]), sub(m[0][0], m[1][1])]

    def project(c):
        inner = [
            [
                pauli(
                    [
                        [
                            (macc[0, 2 * b1 + b0, 2 * a1 + a0], macc[1, 2 * b1 + b0, 2 * a1 + a0])
                            for a0 in range(2)
                        ]
                        for b0 in range(2)
                    ]
                )
                for a1 in range(2)
            ]
            for b1 in range(2)
        ]
        site = lax.broadcasted_iota(jnp.int32, (1, 1024), 1)
        valid = (site < 768) | (c < CHUNKS - 1)
        for low in range(4):
            outer = pauli([[inner[b1][a1][low] for a1 in range(2)] for b1 in range(2)])
            for high in range(4):
                n = 4 * high + low
                for part in range(2):
                    kbuf[pl.ds(16 * part + n, 1), :] = jnp.where(valid, outer[high][part], 0.0)
        result = acc[...]
        dims = (((1,), (1,)), ((), ()))
        for pair in range(4):
            left = kbuf[:, pl.ds(256 * pair, 256)]
            hi = left.astype(jnp.bfloat16)
            lo = (left - hi.astype(F32)).astype(jnp.bfloat16)
            for x, y in ((hi, ph_hi), (lo, ph_hi), (hi, ph_lo)):
                result = result + lax.dot_general(
                    x, y[c, pair], dims, preferred_element_type=F32
                )
        acc[...] = result

    acc[...] = jnp.zeros_like(acc)
    load(prop, sv, s_sem, 0).wait()
    source(0, 0)
    pl.semaphore_wait(barrier, 7)

    def slot(s, carry):
        for parity in range(2):
            @pl.when((s % 2 == parity) & (s < SLOTS))
            def _(parity=parity):
                relay(s, parity)

        for u in range(4):
            @pl.when((s % 4 == u) & (s + 1 < PACKETS))
            def _(u=u):
                if u == 3:
                    for c in range(1, CHUNKS):
                        @pl.when(s + 1 == 4 * c)
                        def _(c=c):
                            load(prop, sv, s_sem, c).wait()
                source((s + 1) // 4, (u + 1) % 4)

        @pl.when(s == PACKETS)
        def _():
            mom[...] = jnp.zeros_like(mom)
            for p in range(NP):
                for i in range(3):
                    mom[i, pl.ds(p, 1), :] = jnp.full((1, 128), momenta[i, p], jnp.int32).astype(F32)
            for c in range(CHUNKS):
                load(back, hv, h_sem, c).wait()

        @pl.when((s > PACKETS) & (s <= PACKETS + CHUNKS))
        def _():
            phases(s - PACKETS - 1)

        @pl.when(s >= FIRST)
        def _():
            t = s - FIRST
            c, al = t // 4, t % 4

            @pl.when(al == 0)
            def _():
                unpack(c)

            contract(c, al)

            @pl.when(al == 3)
            def _():
                project(c)

        return carry

    lax.fori_loop(0, END, slot, 0)
    for s in range(SENDS - OUT_RING, SENDS):
        for d in range(6):
            message(s % 2, s, d).wait_send()

    scale = 0.125 / (72.0 * math.sqrt(L * L * L))
    value = acc[...] * scale
    kr, ki = value[0:16], value[16:32]
    cbuf[0, :, 0:32] = kr[:, 0:32] - ki[:, 32:64]
    cbuf[1, :, 0:32] = kr[:, 32:64] + ki[:, 0:32]
    for current in range(NG):
        g = gtab[current]
        for part in range(2):
            ex[current // 8, part, pl.ds(current % 8, 1), :] = cbuf[part, pl.ds(g, 1), :]
    swap = pltpu.make_async_remote_copy(
        src_ref=ex.at[1 - gz],
        dst_ref=rx,
        send_sem=ex_send,
        recv_sem=ex_recv,
        device_id=(ta, 1 - gz),
        device_id_type=MESH,
    )
    swap.start()
    swap.wait()
    for part in range(2):
        out[part, 0] = (ex[gz, part] + rx[part])[:, 0:NP]


def body(propagator, backward, sink_time, source_position, momenta, gamma_table):
    vmem, smem = pltpu.VMEM, pltpu.SMEM
    tile = (1, 1024)
    return pl.pallas_call(
        kernel,
        out_shape=jax.ShapeDtypeStruct((2, 1, 8, NP), F32),
        in_specs=[pl.BlockSpec(memory_space=pl.ANY)] * 2 + [pl.BlockSpec(memory_space=smem)] * 5,
        out_specs=pl.BlockSpec(memory_space=vmem),
        scratch_shapes=[
            vmem((CHUNKS, 2, 12, 12) + tile, F32),
            vmem((CHUNKS, 2, 12, 12) + tile, F32),
            vmem((CHUNKS, 6, 26) + tile, F32),
            vmem((SLOTS, 6, 7) + tile, F32),
            vmem((6, SLOTS // 2 * 13) + tile, F32),
            vmem((OUT_RING, 6, 7) + tile, F32),
            vmem((3, 78) + tile, F32),
            vmem((3, 12) + tile, F32),
            vmem((12, 12) + tile, F32),
            vmem((2, 4, 4) + tile, F32),
            vmem((32, 1024), F32),
            vmem((CHUNKS, 4, 64, 256), jnp.bfloat16),
            vmem((CHUNKS, 4, 64, 256), jnp.bfloat16),
            vmem((3, 32, 128), F32),
            vmem((32, 64), F32),
            vmem((2, 16, 128), F32),
            vmem((2, 2, 8, 128), F32),
            vmem((2, 8, 128), F32),
            pltpu.SemaphoreType.DMA((CHUNKS,)),
            pltpu.SemaphoreType.DMA((CHUNKS,)),
            pltpu.SemaphoreType.DMA((OUT_RING, 6)),
            pltpu.SemaphoreType.DMA((SEM_RING, 6)),
            pltpu.SemaphoreType.DMA,
            pltpu.SemaphoreType.DMA,
        ],
        compiler_params=pltpu.CompilerParams(
            collective_id=0, has_side_effects=True, vmem_limit_bytes=67_000_000
        ),
    )(
        propagator,
        backward,
        jnp.asarray(tree_words()),
        sink_time,
        source_position,
        jnp.transpose(momenta),
        gamma_table,
    )


def solution(mesh):
    in_specs = (
        P(None, None, None, "ta", "gz"),
        P(None, None, None, "ta", "gz"),
        P(),
        P(),
        P(),
        P(),
    )
    out_specs = P(None, "ta", "gz", None)
    return jax.shard_map(body, mesh=mesh, in_specs=in_specs, out_specs=out_specs, check_vma=False)
```

profile of v0, /device:TPU:1, one launch (start us, length us, event | category | flops | bytes accessed | tf_op | source)
XLA Modules:
  0.0 66.0 jit_solution(18198401376525374319)
XLA Ops:
  0.7 64.0 %shard_map.73 = f32[2,1,8,27]{3,2,1,0:T(8,128)} custom-call(f32[2,12,12,1,6912]{4,3,2,1,0:T(1,128)} %prop.1, f32[2,12,12,1,6912]{4,3,2,1,0:T(1,128)} %back.1, s32[192]{0:T(256)} %constant.2.clone.words, s32[1]{0:T(128)S(6)} %copy.9.sink, s32[3]{0:T(128)} %origin.1, s32[3,27]{1,0:T(4,128)} %bitcast.1, s32[16]{0:T(128)} %gtab.1), custom_call_target="tpu_custom_call" | custom-call | tf_op jit(solution)/shard_map/pallas_call | solution.py:449
  64.7 1.3 %copy.10 = f32[2,1,8,27]{3,2,1,0:T(8,128)} copy(f32[2,1,8,27]{3,2,1,0:T(8,128)} %shard_map.73) | data formatting | bytes 3456
where the time goes:
time: 66.2 us; the launch traced here: 66 us
  Pallas kernels  64 us (97%)
  local copies, waits for them, and re-layouts  1.3 us (2%)
    pallas_call x1, Pallas kernels, body(): pl.pallas_call(kernel, out_shape=jax.ShapeDtypeStruct((2, 1, 8, NP), F32)...  64 us

commit v1 on v0

v1 whole, which is shorter than its diff:
```python
import functools
import itertools
import math

import jax
import jax.numpy as jnp
import numpy as np
from jax import lax
from jax.experimental import pallas as pl
from jax.experimental.pallas import tpu as pltpu
from jax.sharding import PartitionSpec as P

L = 24
NG = 16
NP = 27
CHUNKS = 7
LAG = 6
PACKETS = 4 * CHUNKS
DEPTH = 7
MOST_SLOTS = PACKETS + DEPTH * LAG
LINE = MOST_SLOTS // 2 * 13
OWN = 6 * LINE
OUT_RING = 4
STEPS = ((1, 0, 0), (-1, 0, 0), (0, 1, 0), (0, -1, 0), (0, 0, 1), (0, 0, -1))
TREE_STEPS = (0, 3, 4, 1, 2, 5)
MESH = pl.DeviceIdType.MESH
F32 = jnp.float32


def moved(v, step, sign=1):
    return tuple((a + sign * b) % 4 for a, b in zip(v, step))


def turned(v):
    return tuple((-c) % 4 for c in (v[2], v[0], v[1]))


def turned_step(d):
    return tuple(-c for c in (d[2], d[0], d[1]))


@functools.cache
def tree_words():
    nodes = list(itertools.product(range(4), repeat=3))
    root, child = (0, 0, 0), (1, 0, 0)

    def level(v):
        return sum(min((a - b) % 4, (b - a) % 4) for a, b in zip(v, child))

    def orbit(tail, step):
        while step != (1, 0, 0):
            tail, step = turned(tail), turned_step(step)
        return tail

    taken = orbit(root, (1, 0, 0))
    options = {
        v: [
            (orbit(moved(v, d, -1), d), d)
            for d in STEPS
            if moved(v, d, -1) != root and level(moved(v, d, -1)) < level(v)
        ]
        for v in nodes
        if v not in (root, child)
    }
    match = {}

    def augment(v, seen):
        for key, d in options[v]:
            if key == taken or key in seen:
                continue
            seen.add(key)
            if key not in match or augment(match[key][0], seen):
                match[key] = (v, d)
                return True
        return False

    for v in options:
        assert augment(v, set())
    into = {child: (1, 0, 0)}
    for v, d in match.values():
        into[v] = d
    depth = {root: 0}

    def depth_of(v):
        if v not in depth:
            depth[v] = depth_of(moved(v, into[v], -1)) + 1
        return depth[v]

    edges = [(v, d) for v, d in into.items()]
    depths = {v: depth_of(v) for v in nodes}
    words = np.zeros((3, 64), np.int32)

    def number(v):
        return (v[0] * 4 + v[1]) * 4 + v[2]

    seen_edges = set()
    for k in range(6):
        assert STEPS.index([d for v, d in edges if moved(v, d, -1) == root][0]) == TREE_STEPS[k]
        for v, d in edges:
            n, j = number(v), STEPS.index(d)
            tail = number(moved(v, d, -1))
            assert (tail, j) not in seen_edges
            seen_edges.add((tail, j))
            words[0, n] |= j << (3 * k)
            words[1, tail] |= k << (3 * j)
        for v, n_hops in depths.items():
            assert n_hops <= DEPTH
            words[2, number(v)] |= n_hops << (3 * k)
        edges = [(turned(v), turned_step(d)) for v, d in edges]
        depths = {turned(v): n_hops for v, n_hops in depths.items()}
    return words.reshape(-1)


PAIRS = [(i, j) for i in range(12) for j in range(i, 12)]
PAIR_NUMBER = {p: n for n, p in enumerate(PAIRS)}


def pair_number(i, j):
    return PAIR_NUMBER[(min(i, j), max(i, j))]


def kernel(
    prop, back, sink_in, origin_in, momenta_in, gtab_in, out,
    sv, hv, inbox, stream, outbox, sig, hsum, ssum, macc, kbuf, ph_hi, ph_lo,
    mom, acc, cbuf, ex, rx, words, sink, origin, momenta, gtab,
    s_sem, h_sem, send_sem, recv_sem, ex_send, ex_recv, small_sem,
):
    ta = lax.axis_index("ta")
    gz = lax.axis_index("gz")
    cy, cx, cz = ta // 16, (ta // 4) % 4, ta % 4

    def load(src, dst, sem, c):
        sites = 1024 if c < CHUNKS - 1 else 768
        return pltpu.make_async_copy(
            src.at[:, :, :, :, pl.ds(1024 * c, sites)],
            dst.at[c, :, :, :, :, pl.ds(0, sites)],
            sem.at[c],
        )

    small = [
        pltpu.make_async_copy(src, dst, small_sem.at[i])
        for i, (src, dst) in enumerate(
            ((sink_in, sink), (origin_in, origin), (momenta_in, momenta), (gtab_in, gtab))
        )
    ]
    for copy in small:
        copy.start()
    for c in range(CHUNKS):
        load(prop, sv, s_sem, c).start()
        load(back, hv, h_sem, c).start()

    def neighbour(d):
        x, y, z = STEPS[d]
        return ((cy + y + 4) % 4 * 4 + (cx + x + 4) % 4) * 4 + (cz + z + 4) % 4

    barrier = pltpu.get_barrier_semaphore()
    for d in range(6):
        pl.semaphore_signal(barrier, inc=1, device_id=(neighbour(d), gz), device_id_type=MESH)
    pl.semaphore_signal(barrier, inc=1, device_id=(ta, 1 - gz), device_id_type=MESH)

    for n, word in enumerate(tree_words().tolist()):
        words[n] = jnp.int32(word)
    small[0].wait()
    root = sink[0]
    rel_x = (cx - root // 4 % 4 + 4) % 4
    rel_y = (cy - root // 16 + 4) % 4
    rel_z = (cz - root % 4 + 4) % 4
    rel = (rel_x * 4 + rel_y) * 4 + rel_z
    is_root = rel == 0
    into_word, from_word, depth_word = words[rel], words[64 + rel], words[128 + rel]
    into = [(into_word >> (3 * k)) & 7 for k in range(6)]
    out_of = [(from_word >> (3 * d)) & 7 for d in range(6)]
    depth = [(depth_word >> (3 * k)) & 7 for k in range(6)]

    def source(c, part):
        lo, hi = ((0, 4), (4, 7), (7, 10), (10, 13))[part]
        for k in range(6):
            for n in range(lo, hi):
                i, j = PAIRS[6 * n + k]
                re = im = None
                for m in range(12):
                    a, b = sv[c, 0, i, m], sv[c, 1, i, m]
                    if i == j:
                        r, q = a * a - b * b, a * b
                        q = q + q
                    else:
                        e, f = sv[c, 0, j, m], sv[c, 1, j, m]
                        r, q = a * e - b * f, a * f + b * e
                    re = r if re is None else re + r
                    im = q if im is None else im + q
                at = OWN + 26 * CHUNKS * k + 26 * c + 2 * n
                stream[at] = re
                stream[at + 1] = im

    def phases(chunk, pairs):
        lane = lax.broadcasted_iota(jnp.int32, (32, 128), 1).astype(F32)
        ox, oy, oz = (origin[i].astype(F32) for i in range(3))
        px, py, pz = mom[0], mom[1], mom[2]
        start = (gz * 6912 + chunk * 1024).astype(F32)
        for pair in pairs:
            for half in range(2):
                site = lane[0:8] + (start + (256.0 * pair + 128.0 * half))
                z = jnp.floor((site + 0.5) * (1.0 / 576.0))
                rest = site - z * 576.0
                x = jnp.floor((rest + 0.5) * (1.0 / 24.0))
                y = rest - x * 24.0
                x, y, z = (jnp.concatenate([v] * 4, axis=0) for v in (x - ox, y - oy, z - oz))
                wave = px * x + py * y + pz * z
                wave = wave - 24.0 * jnp.floor(wave * (1.0 / 24.0) + 0.5)
                angle = wave * (math.pi / L)
                square = angle * angle
                s = c = None
                for n in range(13, 0, -2):
                    term = (-1.0) ** (n // 2) / math.factorial(n)
                    s = term if s is None else s * square + term
                for n in range(12, -1, -2):
                    term = (-1.0) ** (n // 2) / math.factorial(n)
                    c = term if c is None else c * square + term
                s = s * angle
                twice = s + s
                for row, value in ((0, 1.0 - twice * s), (32, -(twice * c))):
                    hi = value.astype(jnp.bfloat16)
                    at = (chunk + 1, pair, pl.ds(row, 32), pl.ds(128 * half, 128))
                    ph_hi[at] = hi
                    ph_lo[at] = (value - hi.astype(F32)).astype(jnp.bfloat16)

    def sums(c, src, dst):
        for i in range(12):
            for m in range(12):
                dst[c, i, m] = src[c, 0, i, m] + src[c, 1, i, m]

    def unpack(c, block, base):
        first, last = ((0, 6), (6, 10), (10, 13))[block]
        for n in range(first, last):
            for k in range(6):
                at = base[k] + c * 26 + 2 * n
                sig[6 * n + k] = stream[at] + stream[at + 1]

    def plus(x, y):
        return y if x is None else x + y

    def contract(c, block, base):
        columns = range(3 * block, 3 * block + 3)

        def one(al):
            part = {(a, m): [None] * 3 for a in range(3) for m in columns}
            for k in range(12):
                rows = [3 * al + a for a in range(3)]
                left = [(hv[c, 0, r, k], hv[c, 1, r, k], hsum[c, r, k]) for r in rows]
                for m in columns:
                    n = pair_number(k, m)
                    at = base[n % 6] + c * 26 + n // 6 * 2
                    right = (stream[at], stream[at + 1], sig[n])
                    for a in range(3):
                        for t in range(3):
                            part[a, m][t] = plus(part[a, m][t], left[a][t] * right[t])
            total = [[None] * 3 for _ in range(4)]
            for a in range(3):
                for m in columns:
                    p1, p2, p3 = part[a, m]
                    br, bi = p1 - p2, p3 - (p1 + p2)
                    bound = (br, bi, br - bi)
                    for be in range(4):
                        row = 3 * be + a
                        forward = (sv[c, 0, row, m], sv[c, 1, row, m], ssum[c, row, m])
                        for t in range(3):
                            total[be][t] = plus(total[be][t], forward[t] * bound[t])
            for be in range(4):
                for t in range(3):
                    value = total[be][t]
                    macc[t, be, al] = value if block == 0 else macc[t, be, al] + value

        @pl.loop(0, 2)
        def _(half):
            one(2 * half)
            one(2 * half + 1)

    def add(p, q):
        return (p[0] + q[0], p[1] + q[1])

    def sub(p, q):
        return (p[0] - q[0], p[1] - q[1])

    def pauli(m):
        d = sub(m[0][1], m[1][0])
        return [add(m[0][0], m[1][1]), add(m[1][0], m[0][1]), (-d[1], d[0]), sub(m[0][0], m[1][1])]

    def entry(be, al):
        m0, m1, m2 = macc[0, be, al], macc[1, be, al], macc[2, be, al]
        return (m0 + m1, m2 - (m0 - m1))

    def project(c):
        inner = [
            [
                pauli(
                    [
                        [
                            entry(2 * b1 + b0, 2 * a1 + a0)
                            for a0 in range(2)
                        ]
                        for b0 in range(2)
                    ]
                )
                for a1 in range(2)
            ]
            for b1 in range(2)
        ]
        site = lax.broadcasted_iota(jnp.int32, (1, 1024), 1)
        valid = (site < 768) | (c < CHUNKS - 1)
        for low in range(4):
            outer = pauli([[inner[b1][a1][low] for a1 in range(2)] for b1 in range(2)])
            for high in range(4):
                n = 4 * high + low
                for part in range(2):
                    kbuf[pl.ds(16 * part + n, 1), :] = jnp.where(valid, outer[high][part], 0.0)
        result = acc[...]
        dims = (((1,), (1,)), ((), ()))
        for pair in range(4):
            left = kbuf[:, pl.ds(256 * pair, 256)]
            hi = left.astype(jnp.bfloat16)
            lo = (left - hi.astype(F32)).astype(jnp.bfloat16)
            for x, y in ((hi, ph_hi), (lo, ph_hi), (hi, ph_lo)):
                result = result + lax.dot_general(
                    x, y[c + 1, pair], dims, preferred_element_type=F32
                )
        acc[...] = result

    acc[...] = jnp.zeros_like(acc)
    macc[...] = jnp.zeros_like(macc)
    ph_hi[0] = jnp.zeros((4, 64, 256), jnp.bfloat16)
    ph_lo[0] = jnp.zeros((4, 64, 256), jnp.bfloat16)
    for copy in small[1:]:
        copy.wait()
    mom[...] = jnp.zeros_like(mom)
    for p in range(NP):
        for i in range(3):
            mom[i, pl.ds(p, 1), :] = jnp.full((1, 128), momenta[i, p], jnp.int32).astype(F32)
    load(prop, sv, s_sem, 0).wait()
    source(0, 0)
    pl.semaphore_wait(barrier, 7)

    lag = LAG - 2 * gz
    shift = 13 * LAG // 2 - 13 * gz
    base = [
        jnp.where(is_root, OWN + 26 * CHUNKS * k, LINE * into[k] + depth[k] * shift)
        for k in range(6)
    ]
    line = [sum(jnp.where(out_of[d] == k, LINE * into[k], 0) for k in range(6)) for d in range(6)]
    own_line = [
        jnp.where(is_root, OWN + 26 * CHUNKS * TREE_STEPS.index(d), line[d]) for d in range(6)
    ]

    def message(s, ring, tiles, d=None):
        links = pl.ds(0, 6) if d is None else d
        return pltpu.make_async_remote_copy(
            src_ref=outbox.at[ring, links, pl.ds(0, tiles)],
            dst_ref=inbox.at[s + lag, links, pl.ds(0, tiles)],
            send_sem=send_sem.at[ring],
            recv_sem=recv_sem.at[s + lag],
            device_id=(neighbour(d or 0), gz),
            device_id_type=MESH,
        )

    def arrive(s, ring, tiles, flat):
        message(s - lag, ring, tiles).wait_recv()
        for d in range(6):
            for i in range(tiles):
                stream[LINE * d + flat + i] = inbox[s, d, i]

    def send(s, ring, tiles, flat, first_slots=False):
        if first_slots:
            pl.when(s >= OUT_RING)(message(s - OUT_RING, ring, tiles).wait_send)
        else:
            message(s - OUT_RING, ring, tiles).wait_send()
        at = own_line if first_slots else line
        for d in range(6):
            for i in range(tiles):
                outbox[ring, d, i] = stream[at[d] + flat + i]
        for d in range(6):
            message(s, ring, tiles, d).start()

    @pl.loop(0, CHUNKS)
    def _(g):
        for u in range(4):
            s = 4 * g + u
            slot = (s, u, 7 - u % 2, 26 * g + 13 * (u // 2) + 7 * (u % 2))
            pl.when(s >= lag)(functools.partial(arrive, *slot))
            send(*slot, first_slots=True)
            if u < 3:
                source(g, u + 1)
            else:
                @pl.when(g < CHUNKS - 1)
                def _():
                    for c in range(1, CHUNKS):
                        @pl.when(g + 1 == c)
                        def _(c=c):
                            load(prop, sv, s_sem, c).wait()

                    source(g + 1, 0)
            if u == 2:
                for c in range(CHUNKS):
                    @pl.when(g == c)
                    def _(c=c):
                        load(back, hv, h_sem, c).wait()

            if u % 2 == 0:
                sums(g, *((sv, ssum), (hv, hsum))[u // 2])
            else:
                phases(g, (u - 1, u))

    slot = (PACKETS, 0, 7, PACKETS // 2 * 13)
    arrive(*slot)
    send(*slot)

    @pl.loop(0, DEPTH - DEPTH * gz)
    def _(p):
        for odd in (1, 0):
            s = PACKETS + 2 * p + 2 - odd
            slot = (s, s % OUT_RING, 7 - odd, (PACKETS // 2 + p + 1 - odd) * 13 + 7 * odd)
            arrive(*slot)
            send(*slot)

    @pl.loop(0, CHUNKS)
    def _(c):
        for block in range(4):
            s = DEPTH * lag + 1 + 4 * c + block
            u = (3 + block) % 4
            ring = u + 2 * gz if u < 2 else u - 2 * gz
            odd = u % 2
            pair = DEPTH * LAG // 2 - DEPTH * gz + 2 * c + (1 + block) // 2
            slot = (s, ring, 7 - odd, 13 * pair + 7 * odd)
            pl.when(4 * c + block < PACKETS - 1)(functools.partial(arrive, *slot))
            pl.when(4 * c + block < PACKETS - 1 - lag)(functools.partial(send, *slot))
            if block == 0:
                project(c - 1)
            if block < 3:
                unpack(c, block, base)
            contract(c, block, base)

    project(CHUNKS - 1)
    for ring in range(4):
        s = PACKETS + (DEPTH - 1) * lag - 4 + ring
        message(s, ring, 7 - ring % 2).wait_send()

    scale = 0.125 / (72.0 * math.sqrt(L * L * L))
    value = acc[...] * scale
    kr, ki = value[0:16], value[16:32]
    cbuf[0, :, 0:32] = kr[:, 0:32] - ki[:, 32:64]
    cbuf[1, :, 0:32] = kr[:, 32:64] + ki[:, 0:32]
    for current in range(NG):
        g = gtab[current]
        for part in range(2):
            ex[current // 8, part, pl.ds(current % 8, 1), :] = cbuf[part, pl.ds(g, 1), :]
    swap = pltpu.make_async_remote_copy(
        src_ref=ex.at[1 - gz],
        dst_ref=rx,
        send_sem=ex_send,
        recv_sem=ex_recv,
        device_id=(ta, 1 - gz),
        device_id_type=MESH,
    )
    swap.start()
    swap.wait()
    for part in range(2):
        out[part, 0] = (ex[gz, part] + rx[part])[:, 0:NP]


def body(propagator, backward, sink_time, source_position, momenta, gamma_table):
    vmem, smem = pltpu.VMEM, pltpu.SMEM
    tile = (1, 1024)
    return pl.pallas_call(
        kernel,
        out_shape=jax.ShapeDtypeStruct((2, 1, 8, NP), F32),
        in_specs=[pl.BlockSpec(memory_space=pl.ANY)] * 6,
        out_specs=pl.BlockSpec(memory_space=vmem),
        scratch_shapes=[
            vmem((CHUNKS, 2, 12, 12) + tile, F32),
            vmem((CHUNKS, 2, 12, 12) + tile, F32),
            vmem((MOST_SLOTS, 6, 7) + tile, F32),
            vmem((OWN + 6 * 26 * CHUNKS,) + tile, F32),
            vmem((OUT_RING, 6, 7) + tile, F32),
            vmem((78,) + tile, F32),
            vmem((CHUNKS, 12, 12) + tile, F32),
            vmem((CHUNKS, 12, 12) + tile, F32),
            vmem((3, 4, 4) + tile, F32),
            vmem((32, 1024), F32),
            vmem((CHUNKS + 1, 4, 64, 256), jnp.bfloat16),
            vmem((CHUNKS + 1, 4, 64, 256), jnp.bfloat16),
            vmem((3, 32, 128), F32),
            vmem((32, 64), F32),
            vmem((2, 16, 128), F32),
            vmem((2, 2, 8, 128), F32),
            vmem((2, 8, 128), F32),
            smem((192,), jnp.int32),
            smem((1,), jnp.int32),
            smem((3,), jnp.int32),
            smem((3, NP), jnp.int32),
            smem((NG,), jnp.int32),
            pltpu.SemaphoreType.DMA((CHUNKS,)),
            pltpu.SemaphoreType.DMA((CHUNKS,)),
            pltpu.SemaphoreType.DMA((OUT_RING,)),
            pltpu.SemaphoreType.DMA((MOST_SLOTS,)),
            pltpu.SemaphoreType.DMA,
            pltpu.SemaphoreType.DMA,
            pltpu.SemaphoreType.DMA((4,)),
        ],
        compiler_params=pltpu.CompilerParams(
            collective_id=0, has_side_effects=True, vmem_limit_bytes=67_000_000
        ),
    )(
        propagator,
        backward,
        sink_time,
        source_position,
        jnp.transpose(momenta),
        gamma_table,
    )


def solution(mesh):
    in_specs = (
        P(None, None, None, "ta", "gz"),
        P(None, None, None, "ta", "gz"),
        P(),
        P(),
        P(),
        P(),
    )
    out_specs = P(None, "ta", "gz", None)
    return jax.shard_map(body, mesh=mesh, in_specs=in_specs, out_specs=out_specs, check_vma=False)
```

time: 66.2 us -> 57.3 us (0.87)
  Pallas kernels: 64 us -> 55.2 us
    pallas_call x1, Pallas kernels: 64 us -> 55.2 us  [body(): pl.pallas_call(kernel, out_shape=jax.ShapeDtypeStruct((2, 1, 8, NP), F32)...]
where the time goes in v1:
time: 57.3 us; the launch traced here: 57.2 us
  Pallas kernels  55.2 us (96%)
  local copies, waits for them, and re-layouts  1.3 us (2%)
  between operations  0.66 us (1%)
    pallas_call x1, Pallas kernels, body(): pl.pallas_call(kernel, out_shape=jax.ShapeDtypeStruct((2, 1, 8, NP), F32)...  55.2 us
    unnamed x1, local copies, waits for them, and re-layouts  1.3 us

profile of v1, /device:TPU:1, one launch (start us, length us, event | category | flops | bytes accessed | tf_op | source)
XLA Modules:
  0.0 57.2 jit_solution(5664991402779931421)
XLA Ops:
  0.7 55.2 %shard_map.64 = f32[2,1,8,27]{3,2,1,0:T(8,128)} custom-call(f32[2,12,12,1,6912]{4,3,2,1,0:T(1,128)} %prop.1, f32[2,12,12,1,6912]{4,3,2,1,0:T(1,128)} %back.1, s32[1]{0:T(128)S(6)} %copy.8.sink_in, s32[3]{0:T(128)} %origin_in.1, s32[3,27]{1,0:T(4,128)} %bitcast.1, s32[16]{0:T(128)} %gtab_in.1), custom_call_target="tpu_custom_call" | custom-call | tf_op jit(solution)/shard_map/pallas_call | solution.py:471
  55.9 1.3 %copy.9 = f32[2,1,8,27]{3,2,1,0:T(8,128)} copy(f32[2,1,8,27]{3,2,1,0:T(8,128)} %shard_map.64) | data formatting | bytes 3456

commit v2 on v1

--- a/solution.py
+++ b/solution.py
@@ -122,7 +122,7 @@
 def kernel(
     prop, back, sink_in, origin_in, momenta_in, gtab_in, out,
     sv, hv, inbox, stream, outbox, sig, hsum, ssum, macc, kbuf, ph_hi, ph_lo,
-    mom, acc, cbuf, ex, rx, words, sink, origin, momenta, gtab,
+    mom, acc, cbuf, rx, words, sink, origin, momenta, gtab,
     s_sem, h_sem, send_sem, recv_sem, ex_send, ex_recv, small_sem,
 ):
     ta = lax.axis_index("ta")
@@ -270,10 +270,8 @@
                     value = total[be][t]
                     macc[t, be, al] = value if block == 0 else macc[t, be, al] + value
 
-        @pl.loop(0, 2)
-        def _(half):
-            one(2 * half)
-            one(2 * half + 1)
+        for al in range(4):
+            one(al)
 
     def add(p, q):
         return (p[0] + q[0], p[1] + q[1])
@@ -319,10 +317,10 @@
             left = kbuf[:, pl.ds(256 * pair, 256)]
             hi = left.astype(jnp.bfloat16)
             lo = (left - hi.astype(F32)).astype(jnp.bfloat16)
-            for x, y in ((hi, ph_hi), (lo, ph_hi), (hi, ph_lo)):
-                result = result + lax.dot_general(
-                    x, y[c + 1, pair], dims, preferred_element_type=F32
-                )
+            both = jnp.concatenate([hi, lo], axis=0)
+            main = lax.dot_general(both, ph_hi[c + 1, pair], dims, preferred_element_type=F32)
+            rest = lax.dot_general(hi, ph_lo[c + 1, pair], dims, preferred_element_type=F32)
+            result = result + (main[0:32] + main[32:64] + rest)
         acc[...] = result
 
     acc[...] = jnp.zeros_like(acc)
@@ -442,17 +440,8 @@
         s = PACKETS + (DEPTH - 1) * lag - 4 + ring
         message(s, ring, 7 - ring % 2).wait_send()
 
-    scale = 0.125 / (72.0 * math.sqrt(L * L * L))
-    value = acc[...] * scale
-    kr, ki = value[0:16], value[16:32]
-    cbuf[0, :, 0:32] = kr[:, 0:32] - ki[:, 32:64]
-    cbuf[1, :, 0:32] = kr[:, 32:64] + ki[:, 0:32]
-    for current in range(NG):
-        g = gtab[current]
-        for part in range(2):
-            ex[current // 8, part, pl.ds(current % 8, 1), :] = cbuf[part, pl.ds(g, 1), :]
     swap = pltpu.make_async_remote_copy(
-        src_ref=ex.at[1 - gz],
+        src_ref=acc,
         dst_ref=rx,
         send_sem=ex_send,
         recv_sem=ex_recv,
@@ -461,8 +450,15 @@
     )
     swap.start()
     swap.wait()
-    for part in range(2):
-        out[part, 0] = (ex[gz, part] + rx[part])[:, 0:NP]
+    scale = 0.125 / (72.0 * math.sqrt(L * L * L))
+    value = (acc[...] + rx[...]) * scale
+    kr, ki = value[0:16], value[16:32]
+    cbuf[0, :, 0:32] = kr[:, 0:32] - ki[:, 32:64]
+    cbuf[1, :, 0:32] = kr[:, 32:64] + ki[:, 0:32]
+    for row in range(NG // 2):
+        g = gtab[NG // 2 * gz + row]
+        for part in range(2):
+            out[part, 0, pl.ds(row, 1), :] = cbuf[part, pl.ds(g, 1), 0:NP]
 
 
 def body(propagator, backward, sink_time, source_position, momenta, gamma_table):
@@ -489,8 +485,7 @@
             vmem((3, 32, 128), F32),
             vmem((32, 64), F32),
             vmem((2, 16, 128), F32),
-            vmem((2, 2, 8, 128), F32),
-            vmem((2, 8, 128), F32),
+            vmem((32, 64), F32),
             smem((192,), jnp.int32),
             smem((1,), jnp.int32),
             smem((3,), jnp.int32),

time: 57.3 us -> 56.8 us (level)
  no operation moved by 1% of the time
where the time goes in v2:
time: 56.8 us; the launch traced here: 56.6 us
  Pallas kernels  54.7 us (96%)
  local copies, waits for them, and re-layouts  1.3 us (2%)
  between operations  0.66 us (1%)
    pallas_call x1, Pallas kernels, body(): pl.pallas_call(kernel, out_shape=jax.ShapeDtypeStruct((2, 1, 8, NP), F32)...  54.7 us
    unnamed x1, local copies, waits for them, and re-layouts  1.3 us

profile of v2, /device:TPU:1, one launch (start us, length us, event | category | flops | bytes accessed | tf_op | source)
XLA Modules:
  0.0 56.6 jit_solution(10791715391414500268)
XLA Ops:
  0.7 54.7 %shard_map.64 = f32[2,1,8,27]{3,2,1,0:T(8,128)} custom-call(f32[2,12,12,1,6912]{4,3,2,1,0:T(1,128)} %prop.1, f32[2,12,12,1,6912]{4,3,2,1,0:T(1,128)} %back.1, s32[1]{0:T(128)S(6)} %copy.8.sink_in, s32[3]{0:T(128)} %origin_in.1, s32[3,27]{1,0:T(4,128)} %bitcast.1, s32[16]{0:T(128)} %gtab_in.1), custom_call_target="tpu_custom_call" | custom-call | tf_op jit(solution)/shard_map/pallas_call | solution.py:467
  55.3 1.3 %copy.9 = f32[2,1,8,27]{3,2,1,0:T(8,128)} copy(f32[2,1,8,27]{3,2,1,0:T(8,128)} %shard_map.64) | data formatting | bytes 3456

commit v3 on v2

--- a/solution.py
+++ b/solution.py
@@ -466,7 +466,7 @@
     tile = (1, 1024)
     return pl.pallas_call(
         kernel,
-        out_shape=jax.ShapeDtypeStruct((2, 1, 8, NP), F32),
+        out_shape=pltpu.VMEM((2, 1, 8, NP), F32),
         in_specs=[pl.BlockSpec(memory_space=pl.ANY)] * 6,
         out_specs=pl.BlockSpec(memory_space=vmem),
         scratch_shapes=[
@@ -500,7 +500,7 @@
             pltpu.SemaphoreType.DMA((4,)),
         ],
         compiler_params=pltpu.CompilerParams(
-            collective_id=0, has_side_effects=True, vmem_limit_bytes=67_000_000
+            collective_id=0, has_side_effects=True, vmem_limit_bytes=62_000_000
         ),
     )(
         propagator,

time: 56.8 us -> 55.7 us (0.981)
  local copies, waits for them, and re-layouts: 1.3 us -> 0.6 us
    unnamed x1, local copies, waits for them, and re-layouts: 1.3 us -> 0.6 us
where the time goes in v3:
time: 55.7 us; the launch traced here: 55.5 us
  Pallas kernels  54.3 us (97%)
  between operations  0.66 us (1%)
  local copies, waits for them, and re-layouts  0.6 us (1%)
    pallas_call x1, Pallas kernels, body(): pl.pallas_call(kernel, out_shape=pltpu.VMEM((2, 1, 8, NP), F32), in_specs...  54.3 us

profile of v3, /device:TPU:1, one launch (start us, length us, event | category | flops | bytes accessed | tf_op | source)
XLA Modules:
  0.0 55.5 jit_solution(3960729872482622515)
XLA Ops:
  0.7 54.3 %shard_map.64 = f32[2,1,8,27]{3,2,1,0:T(8,128)S(1)} custom-call(f32[2,12,12,1,6912]{4,3,2,1,0:T(1,128)} %prop.1, f32[2,12,12,1,6912]{4,3,2,1,0:T(1,128)} %back.1, s32[1]{0:T(128)S(6)} %copy.9.sink_in, s32[3]{0:T(128)} %origin_in.1, s32[3,27]{1,0:T(4,128)} %bitcast.1, s32[16]{0:T(128)} %gtab_in.1), custom_call_target="tpu_custom_call" | custom-call | tf_op jit(solution)/shard_map/pallas_call | solution.py:467
  54.9 0.6 %copy.8 = f32[2,1,8,27]{3,2,1,0:T(8,128)} copy(f32[2,1,8,27]{3,2,1,0:T(8,128)S(1)} %shard_map.64) | data formatting | bytes 3456

commit v4 on v3

--- a/solution.py
+++ b/solution.py
@@ -323,16 +323,18 @@
             result = result + (main[0:32] + main[32:64] + rest)
         acc[...] = result
 
-    acc[...] = jnp.zeros_like(acc)
-    macc[...] = jnp.zeros_like(macc)
-    ph_hi[0] = jnp.zeros((4, 64, 256), jnp.bfloat16)
-    ph_lo[0] = jnp.zeros((4, 64, 256), jnp.bfloat16)
-    for copy in small[1:]:
-        copy.wait()
-    mom[...] = jnp.zeros_like(mom)
-    for p in range(NP):
-        for i in range(3):
-            mom[i, pl.ds(p, 1), :] = jnp.full((1, 128), momenta[i, p], jnp.int32).astype(F32)
+    def prepare():
+        acc[...] = jnp.zeros_like(acc)
+        macc[...] = jnp.zeros_like(macc)
+        ph_hi[0] = jnp.zeros((4, 64, 256), jnp.bfloat16)
+        ph_lo[0] = jnp.zeros((4, 64, 256), jnp.bfloat16)
+        for copy in small[1:]:
+            copy.wait()
+        mom[...] = jnp.zeros_like(mom)
+        for p in range(NP):
+            for i in range(3):
+                mom[i, pl.ds(p, 1), :] = jnp.full((1, 128), momenta[i, p], jnp.int32).astype(F32)
+
     load(prop, sv, s_sem, 0).wait()
     source(0, 0)
     pl.semaphore_wait(barrier, 7)
@@ -384,6 +386,8 @@
             slot = (s, u, 7 - u % 2, 26 * g + 13 * (u // 2) + 7 * (u % 2))
             pl.when(s >= lag)(functools.partial(arrive, *slot))
             send(*slot, first_slots=True)
+            if u == 0:
+                pl.when(g == 0)(prepare)
             if u < 3:
                 source(g, u + 1)
             else:

time: 55.7 us -> 55.6 us (level)
  no operation moved by 1% of the time
where the time goes in v4:
time: 55.6 us; the launch traced here: 55.5 us
  Pallas kernels  54.2 us (97%)
  between operations  0.66 us (1%)
  local copies, waits for them, and re-layouts  0.6 us (1%)
    pallas_call x1, Pallas kernels, body(): pl.pallas_call(kernel, out_shape=pltpu.VMEM((2, 1, 8, NP), F32), in_specs...  54.2 us

profile of v4, /device:TPU:1, one launch (start us, length us, event | category | flops | bytes accessed | tf_op | source)
XLA Modules:
  0.0 55.5 jit_solution(7152266548988972369)
XLA Ops:
  0.7 54.2 %shard_map.64 = f32[2,1,8,27]{3,2,1,0:T(8,128)S(1)} custom-call(f32[2,12,12,1,6912]{4,3,2,1,0:T(1,128)} %prop.1, f32[2,12,12,1,6912]{4,3,2,1,0:T(1,128)} %back.1, s32[1]{0:T(128)S(6)} %copy.9.sink_in, s32[3]{0:T(128)} %origin_in.1, s32[3,27]{1,0:T(4,128)} %bitcast.1, s32[16]{0:T(128)} %gtab_in.1), custom_call_target="tpu_custom_call" | custom-call | tf_op jit(solution)/shard_map/pallas_call | solution.py:471
  54.9 0.6 %copy.8 = f32[2,1,8,27]{3,2,1,0:T(8,128)} copy(f32[2,1,8,27]{3,2,1,0:T(8,128)S(1)} %shard_map.64) | data formatting | bytes 3456
